TPU v7x, 128 devices: a whole 4x4x4 slice. The times are simulated.
128 devices in a mesh: rows: 4 (over z), cols: 8 (over y_hi, x), slabs: 4 (over y_lo, core).
Axes of the slice: x: 4, y: 4 (y_hi: 2, y_lo: 2; y = y_hi * 2 + y_lo), z: 4, core: 2. Of those that a mesh axis runs over, the one named last changes fastest.
Arguments:
- tracer: float32 [16, 512, 256, 128], P('rows', 'cols', 'slabs'), may hold values from 0.2 to 1.8
- crowding: float32 [16, 512, 256, 128], P('rows', 'cols', 'slabs'), may hold values from 0.5 to 2
Outputs:
- column_sum: float32 [16, 512, 256, 128], P('rows', 'cols', 'slabs')
- tracer_end: float32 [16, 512, 256, 128], P('rows', 'cols', 'slabs')
All inputs are finite; a program needn't handle non-finite values.
Results may differ from a plain program's by a relative error of at most 0.00002.
Values sent between devices are 32-bit elements; how exact they have to be, the bound alone decides.
A program may use at most 320 MiB of HBM per device.

v0:
```python
import jax
import jax.numpy as jnp
from jax import lax
from jax.sharding import PartitionSpec as P

STEPS = 4


def extended(array, sides, width):
    edges = {}
    for axis, dim in sides:
        count, length = (lax.axis_size(axis), array.shape[dim])
        up = [(i, (i + 1) % count) for i in range(count - 1)]
        last = lax.slice_in_dim(array, length - width, length, axis=dim)
        initial = lax.slice_in_dim(array, 0, width, axis=dim)
        edges[dim] = (
            lax.ppermute(last, axis, up),
            lax.ppermute(initial, axis, [(b, a) for a, b in up]),
        )
    done = []
    for _, dim in sides:
        low, high = edges[dim]
        around = [(width, width) if d in done else (0, 0) for d in range(array.ndim)]
        array = jnp.concatenate([jnp.pad(low, around), array, jnp.pad(high, around)], axis=dim)
        done.append(dim)
    return array


def prefix(array, axis, combine, identity):
    count, place = (lax.axis_size(axis), lax.axis_index(axis))
    everything = lax.all_gather(array, axis)
    start = jnp.broadcast_to(jnp.asarray(identity, array.dtype), array.shape)

    def turn(k, before):
        reached = k < place
        new = combine(before, everything[k])
        return jnp.where(reached, new, before)

    return lax.fori_loop(0, count, turn, start)


def inner_cells(values, dims):
    for dim in dims:
        values = lax.slice_in_dim(values, 1, values.shape[dim] - 1, axis=dim)
    return values


def side_cells(values, dim, start, dims):
    others = [other for other in dims if other != dim]
    values = inner_cells(values, others)
    return lax.slice_in_dim(values, start, start + values.shape[dim] - 2, axis=dim)


def advance(padded, crowding):
    middle = inner_cells(padded, (0, 1, 2))
    lower = [side_cells(padded, dim, 0, (0, 1, 2)) for dim in (0, 1, 2)]
    upper = [side_cells(padded, dim, 2, (0, 1, 2)) for dim in (0, 1, 2)]
    spread = lower[0] + upper[0] + lower[1] + upper[1] + lower[2] + upper[2] - 6.0 * middle
    return middle + 0.1 * spread + 0.2 * middle * (1.0 - middle * crowding)


def body(tracer, crowding):
    for step in range(STEPS):
        padded = extended(tracer, (("rows", 0), ("cols", 1), ("slabs", 2)), 1)
        tracer = advance(padded, crowding)
    here = jnp.cumsum(tracer, axis=0)
    total = lax.slice_in_dim(here, here.shape[0] - 1, here.shape[0], axis=0)

    def add_pair(earlier_total, later_total):
        return earlier_total + later_total

    below = prefix(total, "rows", add_pair, jnp.zeros_like(total))
    column_sum = (here + below) / (tracer.shape[0] * lax.axis_size("rows"))
    return (column_sum, tracer)


def solution(mesh):
    placed = (P("rows", "cols", "slabs", None), P("rows", "cols", "slabs", None))
    return jax.shard_map(
        body,
        mesh=mesh,
        in_specs=placed,
        out_specs=(P("rows", "cols", "slabs", None), P("rows", "cols", "slabs", None)),
        check_vma=False,
    )
```

profile of v0, /device:TPU:68, one launch (start us, length us, event | category | flops | bytes accessed | tf_op | source)
XLA Modules:
  0.0 446.2 jit_solution(17947315886823089585)
XLA Ops:
  7.2 2.5 fusion.55
  9.7 3.5 collective-permute-start
  13.3 2.3 collective-permute-start.1
  16.6 3.1 collective-permute-start.2
  19.7 2.7 collective-permute-start.3
  22.5 1.7 fusion.53
  27.7 31.3 %collective-permute-done = f32[1,64,64,128]{3,2,1,0:T(8,128)S(1)} collective-permute-done((f32[1,64,64,128]{3,2,1,0:T(8,128)S(1)}, f32[1,64,64,128]{3,2,1,0:T(8,128)S(1)}, u32[]{:S(2)}, u32[]{:S(2)}) %collective-permute-start) | collective-permute-done | bytes 2097184 | tf_op jit(solution)/shard_map/ppermute | solution.py:17
  60.6 8.9 %constant_dynamic-update-slice_fusion.1 = f32[6,64,64,128]{3,2,1,0:T(8,128)} fusion(f32[6,64,64,128]{3,2,1,0:T(8,128)} %constant_dynamic-update-slice_fusion.2, f32[4,64,64,128]{3,2,1,0:T(8,128)} %param.4), kind=kLoop, calls=%fused_computation.113 | loop fusion | bytes 16777216
  71.1 22.7 %fusion.38 = f32[4,64,64,128]{3,2,1,0:T(8,128)} fusion(f32[4,64,64,128]{3,2,1,0:T(8,128)} %param.4, f32[4,64,1,128]{3,2,1,0:T(1,128)S(1)} %bitcast.33, f32[6,1,64,128]{3,2,1,0:T(8,128)S(1)} %pad.51, f32[6,64,64,128]{3,2,1,0:T(8,128)} %constant_dynamic-update-slice_fusion, f32[6,1,64,128]{3,2,1,0:T(8,128)S(1)} %pad.50, f32[4,64,1,128]{3,2,1,0:T(1,128)S(1)} %bitcast.29, ...), kind=kLoop, calls=%fused_computation.94 | loop fusion | flops 62914560 | bytes 42598400 | tf_op jit(solution)/shard_map/add | solution.py:59
  93.8 2.5 fusion.51
  96.3 3.5 collective-permute-start.6
  99.9 2.3 collective-permute-start.7
  103.2 3.1 collective-permute-start.8
  106.3 2.7 collective-permute-start.9
  109.1 1.7 fusion.50
  114.3 2.9 collective-permute-done.11
  117.2 27.6 %collective-permute-done.6 = f32[1,64,64,128]{3,2,1,0:T(8,128)S(1)} collective-permute-done((f32[1,64,64,128]{3,2,1,0:T(8,128)S(1)}, f32[1,64,64,128]{3,2,1,0:T(8,128)S(1)}, u32[]{:S(2)}, u32[]{:S(2)}) %collective-permute-start.6) | collective-permute-done | bytes 2097184 | tf_op jit(solution)/shard_map/ppermute | solution.py:17
  144.8 3.3 collective-permute-done.7
  148.0 24.8 %fusion.27 = f32[4,64,64,128]{3,2,1,0:T(8,128)} fusion(f32[4,64,64,128]{3,2,1,0:T(8,128)} %fusion.38, f32[4,64,1,128]{3,2,1,0:T(1,128)S(1)} %bitcast.35, f32[6,1,64,128]{3,2,1,0:T(8,128)S(1)} %pad.55, f32[6,1,64,128]{3,2,1,0:T(8,128)S(1)} %pad.54, f32[1,64,64,128]{3,2,1,0:T(8,128)S(1)} %collective-permute-done.7, ...), kind=kLoop, calls=%fused_computation.65 | loop fusion | flops 79691776 | bytes 30015488 | tf_op jit(solution)/shard_map/add | solution.py:59
  172.8 2.5 fusion.48
  175.4 1.9 collective-permute-start.12
  177.3 3.9 collective-permute-start.13
  182.2 3.1 collective-permute-start.14
  185.3 2.7 collective-permute-start.15
  188.1 1.7 fusion.47
  193.3 2.9 collective-permute-done.17
  196.2 26.4 %collective-permute-done.12 = f32[1,64,64,128]{3,2,1,0:T(8,128)S(1)} collective-permute-done((f32[1,64,64,128]{3,2,1,0:T(8,128)S(1)}, f32[1,64,64,128]{3,2,1,0:T(8,128)S(1)}, u32[]{:S(2)}, u32[]{:S(2)}) %collective-permute-start.12) | collective-permute-done | bytes 2097184 | tf_op jit(solution)/shard_map/ppermute | solution.py:17
  222.6 1.9 collective-permute-done.13
  224.6 24.6 %fusion.16 = f32[4,64,64,128]{3,2,1,0:T(8,128)} fusion(f32[4,64,64,128]{3,2,1,0:T(8,128)} %fusion.27, f32[4,64,1,128]{3,2,1,0:T(1,128)S(1)} %bitcast.36, f32[6,1,64,128]{3,2,1,0:T(8,128)S(1)} %pad.59, f32[6,1,64,128]{3,2,1,0:T(8,128)S(1)} %pad.58, f32[1,64,64,128]{3,2,1,0:T(8,128)S(1)} %collective-permute-done.13, ...), kind=kLoop, calls=%fused_computation.36 | loop fusion | flops 79691776 | bytes 30015488 | tf_op jit(solution)/shard_map/add | solution.py:59
  249.2 2.5 fusion.45
  251.7 1.9 collective-permute-start.18
  253.6 3.9 collective-permute-start.19
  258.6 3.1 collective-permute-start.20
  261.7 2.7 collective-permute-start.21
  264.4 1.7 fusion.44
  267.5 3.0 collective-permute-start.22
  271.5 26.6 %collective-permute-done.18 = f32[1,64,64,128]{3,2,1,0:T(8,128)S(1)} collective-permute-done((f32[1,64,64,128]{3,2,1,0:T(8,128)S(1)}, f32[1,64,64,128]{3,2,1,0:T(8,128)S(1)}, u32[]{:S(2)}, u32[]{:S(2)}) %collective-permute-start.18) | collective-permute-done | bytes 2097184 | tf_op jit(solution)/shard_map/ppermute | solution.py:17
  298.1 1.9 collective-permute-done.19
  300.1 24.8 %fusion.5 = f32[4,64,64,128]{3,2,1,0:T(8,128)} fusion(f32[4,64,64,128]{3,2,1,0:T(8,128)} %fusion.16, f32[4,64,1,128]{3,2,1,0:T(1,128)S(1)} %bitcast.30, f32[6,1,64,128]{3,2,1,0:T(8,128)S(1)} %pad.63, f32[6,1,64,128]{3,2,1,0:T(8,128)S(1)} %pad.62, f32[1,64,64,128]{3,2,1,0:T(8,128)S(1)} %collective-permute-done.19, ...), kind=kLoop, calls=%fused_computation.7 | loop fusion | flops 79691776 | bytes 30015488 | tf_op jit(solution)/shard_map/add | solution.py:59
  324.9 8.7 %fusion.56 = f32[4,64,64,128]{3,2,1,0:T(8,128)} fusion(f32[4,64,64,128]{3,2,1,0:T(8,128)} %fusion.5), kind=kOutput, calls=%fused_computation.127 | output fusion | flops 6291456 | bytes 16777216 | tf_op jit(solution)/shard_map/jit(cumsum)/reduce_window_sum | solution.py:66
  333.6 3.2 slice.370
  336.8 84.4 %all-gather.3.cloned.1.call-done = f32[4,64,64,128]{3,2,1,0:T(8,128)} async-done(((f32[1,64,64,128]{3,2,1,0:T(8,128)}), f32[4,64,64,128]{3,2,1,0:T(8,128)}) %all-gather.3.cloned.1.call-update) | async-done | bytes 8388624 | tf_op jit(solution)/shard_map/all_gather | solution.py:31
  421.2 9.3 %while.14 = (s32[]{:T(128)}, f32[1,64,64,128]{3,2,1,0:T(8,128)S(1)}, s32[]{:T(128)}, f32[4,1,64,64,128]{4,3,2,1,0:T(8,128)}, s32[]{:T(128)}, /*index=5*/s32[]{:T(128)}) while((s32[]{:T(128)}, f32[1,64,64,128]{3,2,1,0:T(8,128)S(1)}, s32[]{:T(128)}, f32[4,1,64,64,128]{4,3,2,1,0:T(8,128)}, s32[]{:T(128)}, /*index=5*/s32[]{:T(128)}) %tuple.57), condition=%wide.region_2.3_spmd.clone, body=%wide.region_1.2_spmd.clone.sunk | while | flops 1572868 | bytes 6291549 | solution.py:39
  421.2 2.3 add_select_fusion.2
  423.6 2.3 add_select_fusion.2
  425.9 2.3 add_select_fusion.2
  428.2 2.3 add_select_fusion.2
  430.6 8.8 %add_multiply_fusion = f32[4,64,64,128]{3,2,1,0:T(8,128)} fusion(f32[4,64,64,128]{3,2,1,0:T(8,128)} %fusion.56, f32[64,64,128]{2,1,0:T(8,128)S(1)} %bitcast.27), kind=kLoop, calls=%fused_computation.111 | loop fusion | flops 4194304 | bytes 18874368 | tf_op jit(solution)/shard_map/div | solution.py:73
  (44 shorter events, 19.8 us)
Async XLA Ops:
  7.2 414.1 %all-gather.3.cloned.1.call-start = ((), (), s32[]{:S(2)}) async-start(), calls=%async_computation | async-start | bytes 10485760 | tf_op jit(solution)/shard_map/all_gather | solution.py:31
  9.7 49.3 %collective-permute-start = (f32[1,64,64,128]{3,2,1,0:T(8,128)S(1)}, f32[1,64,64,128]{3,2,1,0:T(8,128)S(1)}, u32[]{:S(2)}, u32[]{:S(2)}) collective-permute-start(f32[1,64,64,128]{3,2,1,0:T(8,128)S(1)} %get-tuple-element.142), channel_id=1, source_target_pairs={{0,32},{32,64},{64,96},{1,33},{33,65},{65,97},{2,34},{34,66},{66,9... | collective-permute-start | bytes 6291464 | tf_op jit(solution)/shard_map/ppermute | solution.py:17
  13.3 56.2 %collective-permute-start.1 = (f32[1,64,64,128]{3,2,1,0:T(8,128)S(1)}, f32[1,64,64,128]{3,2,1,0:T(8,128)S(1)}, u32[]{:S(2)}, u32[]{:S(2)}) collective-permute-start(f32[1,64,64,128]{3,2,1,0:T(8,128)S(1)} %get-tuple-element.141), channel_id=1, source_target_pairs={{32,0},{64,32},{96,64},{33,1},{65,33},{97,65},{34,2},{66,34},{98,6... | collective-permute-start | bytes 6291464 | tf_op jit(solution)/shard_map/ppermute | solution.py:18
  16.6 8.9 %collective-permute-start.2 = (f32[4,1,64,128]{3,2,1,0:T(8,128)S(1)}, f32[4,1,64,128]{3,2,1,0:T(8,128)S(1)}, u32[]{:S(2)}, u32[]{:S(2)}) collective-permute-start(f32[4,1,64,128]{3,2,1,0:T(8,128)S(1)} %get-tuple-element.139), channel_id=1, source_target_pairs={{0,4},{4,8},{8,12},{12,16},{16,20},{20,24},{24,28},{1,5},{5,9},{9,... | collective-permute-start | bytes 393224 | tf_op jit(solution)/shard_map/ppermute | solution.py:17
  19.7 8.0 %collective-permute-start.3 = (f32[4,1,64,128]{3,2,1,0:T(8,128)S(1)}, f32[4,1,64,128]{3,2,1,0:T(8,128)S(1)}, u32[]{:S(2)}, u32[]{:S(2)}) collective-permute-start(f32[4,1,64,128]{3,2,1,0:T(8,128)S(1)} %get-tuple-element.140), channel_id=1, source_target_pairs={{4,0},{8,4},{12,8},{16,12},{20,16},{24,20},{28,24},{5,1},{9,5},{13... | collective-permute-start | bytes 393224 | tf_op jit(solution)/shard_map/ppermute | solution.py:18
  24.2 46.9 %collective-permute-start.4 = (f32[4,64,1,128]{3,1,2,0:T(8,128)S(1)}, f32[4,64,1,128]{3,1,2,0:T(8,128)S(1)}, u32[]{:S(2)}, u32[]{:S(2)}) collective-permute-start(f32[4,64,1,128]{3,1,2,0:T(8,128)S(1)} %bitcast.38), channel_id=1, source_target_pairs={{0,1},{1,2},{2,3},{4,5},{5,6},{6,7},{8,9},{9,10},{10,11},{12,13},{... | collective-permute-start | bytes 393224 | tf_op jit(solution)/shard_map/ppermute | solution.py:17
  25.5 45.6 %collective-permute-start.5 = (f32[4,64,1,128]{3,1,2,0:T(8,128)S(1)}, f32[4,64,1,128]{3,1,2,0:T(8,128)S(1)}, u32[]{:S(2)}, u32[]{:S(2)}) collective-permute-start(f32[4,64,1,128]{3,1,2,0:T(8,128)S(1)} %bitcast.37), channel_id=1, source_target_pairs={{1,0},{2,1},{3,2},{5,4},{6,5},{7,6},{9,8},{10,9},{11,10},{13,12},{... | collective-permute-start | bytes 393224 | tf_op jit(solution)/shard_map/ppermute | solution.py:18
  59.0 12.1 %slice-start = ((s8[8388608]{0:T(1024)(128)(4,1)}), s8[4194304]{0:T(1024)(128)(4,1)S(1)}, s32[]{:S(2)}) async-start(s8[8388608]{0:T(1024)(128)(4,1)} %bitcast.25), calls=%async_computation.1 | async-start | bytes 8388608
  60.6 10.5 %slice-start.1 = ((s8[8388608]{0:T(1024)(128)(4,1)}), s8[4194304]{0:T(1024)(128)(4,1)S(1)}, s32[]{:S(2)}) async-start(s8[8388608]{0:T(1024)(128)(4,1)} %bitcast.25), calls=%async_computation.2 | async-start | bytes 8388608
  96.3 48.4 %collective-permute-start.6 = (f32[1,64,64,128]{3,2,1,0:T(8,128)S(1)}, f32[1,64,64,128]{3,2,1,0:T(8,128)S(1)}, u32[]{:S(2)}, u32[]{:S(2)}) collective-permute-start(f32[1,64,64,128]{3,2,1,0:T(8,128)S(1)} %get-tuple-element.133), channel_id=1, source_target_pairs={{0,32},{32,64},{64,96},{1,33},{33,65},{65,97},{2,34},{34,66},{66,9... | collective-permute-start | bytes 6291464 | tf_op jit(solution)/shard_map/ppermute | solution.py:17
  99.9 48.1 %collective-permute-start.7 = (f32[1,64,64,128]{3,2,1,0:T(8,128)S(1)}, f32[1,64,64,128]{3,2,1,0:T(8,128)S(1)}, u32[]{:S(2)}, u32[]{:S(2)}) collective-permute-start(f32[1,64,64,128]{3,2,1,0:T(8,128)S(1)} %get-tuple-element.134), channel_id=1, source_target_pairs={{32,0},{64,32},{96,64},{33,1},{65,33},{97,65},{34,2},{66,34},{98,6... | collective-permute-start | bytes 6291464 | tf_op jit(solution)/shard_map/ppermute | solution.py:18
  103.2 8.9 %collective-permute-start.8 = (f32[4,1,64,128]{3,2,1,0:T(8,128)S(1)}, f32[4,1,64,128]{3,2,1,0:T(8,128)S(1)}, u32[]{:S(2)}, u32[]{:S(2)}) collective-permute-start(f32[4,1,64,128]{3,2,1,0:T(8,128)S(1)} %get-tuple-element.135), channel_id=1, source_target_pairs={{0,4},{4,8},{8,12},{12,16},{16,20},{20,24},{24,28},{1,5},{5,9},{9,... | collective-permute-start | bytes 393224 | tf_op jit(solution)/shard_map/ppermute | solution.py:17
  106.3 8.0 %collective-permute-start.9 = (f32[4,1,64,128]{3,2,1,0:T(8,128)S(1)}, f32[4,1,64,128]{3,2,1,0:T(8,128)S(1)}, u32[]{:S(2)}, u32[]{:S(2)}) collective-permute-start(f32[4,1,64,128]{3,2,1,0:T(8,128)S(1)} %get-tuple-element.136), channel_id=1, source_target_pairs={{4,0},{8,4},{12,8},{16,12},{20,16},{24,20},{28,24},{5,1},{9,5},{13... | collective-permute-start | bytes 393224 | tf_op jit(solution)/shard_map/ppermute | solution.py:18
  110.8 3.5 collective-permute-start.10
  112.1 5.0 %collective-permute-start.11 = (f32[4,64,1,128]{3,1,2,0:T(8,128)S(1)}, f32[4,64,1,128]{3,1,2,0:T(8,128)S(1)}, u32[]{:S(2)}, u32[]{:S(2)}) collective-permute-start(f32[4,64,1,128]{3,1,2,0:T(8,128)S(1)} %bitcast.40), channel_id=1, source_target_pairs={{1,0},{2,1},{3,2},{5,4},{6,5},{7,6},{9,8},{10,9},{11,10},{13,12},{... | collective-permute-start | bytes 393224 | tf_op jit(solution)/shard_map/ppermute | solution.py:18
  175.4 47.3 %collective-permute-start.12 = (f32[1,64,64,128]{3,2,1,0:T(8,128)S(1)}, f32[1,64,64,128]{3,2,1,0:T(8,128)S(1)}, u32[]{:S(2)}, u32[]{:S(2)}) collective-permute-start(f32[1,64,64,128]{3,2,1,0:T(8,128)S(1)} %get-tuple-element.127), channel_id=1, source_target_pairs={{0,32},{32,64},{64,96},{1,33},{33,65},{65,97},{2,34},{34,66},{66,9... | collective-permute-start | bytes 6291464 | tf_op jit(solution)/shard_map/ppermute | solution.py:17
  177.3 47.3 %collective-permute-start.13 = (f32[1,64,64,128]{3,2,1,0:T(8,128)S(1)}, f32[1,64,64,128]{3,2,1,0:T(8,128)S(1)}, u32[]{:S(2)}, u32[]{:S(2)}) collective-permute-start(f32[1,64,64,128]{3,2,1,0:T(8,128)S(1)} %get-tuple-element.128), channel_id=1, source_target_pairs={{32,0},{64,32},{96,64},{33,1},{65,33},{97,65},{34,2},{66,34},{98,6... | collective-permute-start | bytes 6291464 | tf_op jit(solution)/shard_map/ppermute | solution.py:18
  182.2 8.9 %collective-permute-start.14 = (f32[4,1,64,128]{3,2,1,0:T(8,128)S(1)}, f32[4,1,64,128]{3,2,1,0:T(8,128)S(1)}, u32[]{:S(2)}, u32[]{:S(2)}) collective-permute-start(f32[4,1,64,128]{3,2,1,0:T(8,128)S(1)} %get-tuple-element.129), channel_id=1, source_target_pairs={{0,4},{4,8},{8,12},{12,16},{16,20},{20,24},{24,28},{1,5},{5,9},{9,... | collective-permute-start | bytes 393224 | tf_op jit(solution)/shard_map/ppermute | solution.py:17
  185.3 8.0 %collective-permute-start.15 = (f32[4,1,64,128]{3,2,1,0:T(8,128)S(1)}, f32[4,1,64,128]{3,2,1,0:T(8,128)S(1)}, u32[]{:S(2)}, u32[]{:S(2)}) collective-permute-start(f32[4,1,64,128]{3,2,1,0:T(8,128)S(1)} %get-tuple-element.130), channel_id=1, source_target_pairs={{4,0},{8,4},{12,8},{16,12},{20,16},{24,20},{28,24},{5,1},{9,5},{13... | collective-permute-start | bytes 393224 | tf_op jit(solution)/shard_map/ppermute | solution.py:18
  189.8 3.5 collective-permute-start.16
  191.2 5.0 %collective-permute-start.17 = (f32[4,64,1,128]{3,1,2,0:T(8,128)S(1)}, f32[4,64,1,128]{3,1,2,0:T(8,128)S(1)}, u32[]{:S(2)}, u32[]{:S(2)}) collective-permute-start(f32[4,64,1,128]{3,1,2,0:T(8,128)S(1)} %bitcast.41), channel_id=1, source_target_pairs={{1,0},{2,1},{3,2},{5,4},{6,5},{7,6},{9,8},{10,9},{11,10},{13,12},{... | collective-permute-start | bytes 393224 | tf_op jit(solution)/shard_map/ppermute | solution.py:18
  251.7 46.4 %collective-permute-start.18 = (f32[1,64,64,128]{3,2,1,0:T(8,128)S(1)}, f32[1,64,64,128]{3,2,1,0:T(8,128)S(1)}, u32[]{:S(2)}, u32[]{:S(2)}) collective-permute-start(f32[1,64,64,128]{3,2,1,0:T(8,128)S(1)} %get-tuple-element.121), channel_id=1, source_target_pairs={{0,32},{32,64},{64,96},{1,33},{33,65},{65,97},{2,34},{34,66},{66,9... | collective-permute-start | bytes 6291464 | tf_op jit(solution)/shard_map/ppermute | solution.py:17
  253.6 46.4 %collective-permute-start.19 = (f32[1,64,64,128]{3,2,1,0:T(8,128)S(1)}, f32[1,64,64,128]{3,2,1,0:T(8,128)S(1)}, u32[]{:S(2)}, u32[]{:S(2)}) collective-permute-start(f32[1,64,64,128]{3,2,1,0:T(8,128)S(1)} %get-tuple-element.122), channel_id=1, source_target_pairs={{32,0},{64,32},{96,64},{33,1},{65,33},{97,65},{34,2},{66,34},{98,6... | collective-permute-start | bytes 6291464 | tf_op jit(solution)/shard_map/ppermute | solution.py:18
  258.6 8.9 %collective-permute-start.20 = (f32[4,1,64,128]{3,2,1,0:T(8,128)S(1)}, f32[4,1,64,128]{3,2,1,0:T(8,128)S(1)}, u32[]{:S(2)}, u32[]{:S(2)}) collective-permute-start(f32[4,1,64,128]{3,2,1,0:T(8,128)S(1)} %get-tuple-element.123), channel_id=1, source_target_pairs={{0,4},{4,8},{8,12},{12,16},{16,20},{20,24},{24,28},{1,5},{5,9},{9,... | collective-permute-start | bytes 393224 | tf_op jit(solution)/shard_map/ppermute | solution.py:17
  261.7 8.9 %collective-permute-start.21 = (f32[4,1,64,128]{3,2,1,0:T(8,128)S(1)}, f32[4,1,64,128]{3,2,1,0:T(8,128)S(1)}, u32[]{:S(2)}, u32[]{:S(2)}) collective-permute-start(f32[4,1,64,128]{3,2,1,0:T(8,128)S(1)} %get-tuple-element.124), channel_id=1, source_target_pairs={{4,0},{8,4},{12,8},{16,12},{20,16},{24,20},{28,24},{5,1},{9,5},{13... | collective-permute-start | bytes 393224 | tf_op jit(solution)/shard_map/ppermute | solution.py:18
  266.2 4.4 collective-permute-start.23
  267.5 4.0 collective-permute-start.22
Sparse Core Ops, SparseCore 0:
  336.9 84.2 all-gather.2
where the time goes:
time: 449 us; the launch traced here: 446 us
  waiting for transfers between devices  212 us (47%)
  other arithmetic  124 us (28%)
  starting transfers between devices  59.1 us (13%)
  local copies, waits for them, and re-layouts  36.5 us (8%)
  between operations  14.4 us (3%)
    ppermute x12, waiting for transfers between devices, extended(): lax.ppermute(last, axis, up)  113 us
    add x4, other arithmetic, advance(): return middle + 0.1 * spread + 0.2 * middle * (1.0 - middle * crowding)  96.9 us
    all_gather x1, waiting for transfers between devices, prefix(): everything = lax.all_gather(array, axis)  84.4 us
    ppermute x12, starting transfers between devices, extended(): lax.ppermute(last, axis, up)  30.3 us
    ppermute x12, starting transfers between devices, extended(): lax.ppermute(initial, axis, [(b, a) for a, b in up])  28.8 us
    slice x11, local copies, waits for them, and re-layouts, extended(): last = lax.slice_in_dim(array, length - width, length, axis=dim)  18.5 us
    ppermute x12, waiting for transfers between devices, extended(): lax.ppermute(initial, axis, [(b, a) for a, b in up])  15.2 us
    unnamed x6, local copies, waits for them, and re-layouts  10.5 us
  transfers between devices with their start and end apart: 25, of which 14 were waited for; matrix products, arithmetic and copies ran while one was open for 5% of the time, Pallas kernels for 0%

commit v1 on v0

v1 whole, which is shorter than its diff:
```python
import functools

import jax
import jax.numpy as jnp
from jax import lax
from jax.experimental import pallas as pl
from jax.experimental.pallas import tpu as pltpu
from jax.sharding import PartitionSpec as P

STEPS = 4
CHUNKS = 8
MESH = pl.DeviceIdType.MESH


def kernel(sizes, tr, cr, out_c, out_t, other, ylo, yhi, xlo, xhi, zlo, zhi, zsl, zsh, q, g,
           load_sem, yu_s, yu_r, yd_s, yd_r, xs, xr, zs, zr, qs, qr):
    rows, cols, slabs = sizes
    ny, nx, nz, nl = tr.shape
    width = nx // CHUNKS
    row, col, slab = (lax.axis_index(a) for a in ("rows", "cols", "slabs"))
    has_up, has_dn = row < rows - 1, row > 0
    has_xu, has_xd = col < cols - 1, col > 0
    has_zu, has_zd = slab < slabs - 1, slab > 0
    fields = (out_t, other)
    first = lax.broadcasted_iota(jnp.int32, (nz, nl), 0) == 0
    final = lax.broadcasted_iota(jnp.int32, (nz, nl), 0) == nz - 1
    inner = jnp.where(has_dn, jnp.float32(0.1), jnp.float32(0.0))

    def chunk(k):
        return pl.ds(pl.multiple_of(k * width, width), width)

    def remote(src, dst, send, recv, axis, index):
        return pltpu.make_async_remote_copy(
            src_ref=src, dst_ref=dst, send_sem=send, recv_sem=recv,
            device_id={axis: index}, device_id_type=MESH)

    up, dn = jnp.minimum(row + 1, rows - 1), jnp.maximum(row - 1, 0)
    xu, xd = jnp.minimum(col + 1, cols - 1), jnp.maximum(col - 1, 0)
    zu, zd = jnp.minimum(slab + 1, slabs - 1), jnp.maximum(slab - 1, 0)

    def y_up(n, k):
        src = tr if n == 0 else fields[n % 2]
        return remote(src.at[ny - 1, chunk(k)], ylo.at[n % 2, chunk(k)], yu_s.at[n, k], yu_r.at[n, k], "rows", up)

    def y_dn(n, k):
        src = tr if n == 0 else fields[n % 2]
        return remote(src.at[0, chunk(k)], yhi.at[n % 2, chunk(k)], yd_s.at[n, k], yd_r.at[n, k], "rows", dn)

    def x_up(n):
        return remote(fields[n % 2].at[:, nx - 1], xlo.at[n % 2], xs.at[n, 0], xr.at[n, 0], "cols", xu)

    def x_dn(n):
        return remote(fields[n % 2].at[:, 0], xhi.at[n % 2], xs.at[n, 1], xr.at[n, 1], "cols", xd)

    def z_up(n):
        return remote(zsh.at[n % 2], zlo.at[n % 2], zs.at[n, 0], zr.at[n, 0], "slabs", zu)

    def z_dn(n):
        return remote(zsl.at[n % 2], zhi.at[n % 2], zs.at[n, 1], zr.at[n, 1], "slabs", zd)

    def q_up(k):
        return remote(g.at[chunk(k)], q.at[chunk(k)], qs.at[k], qr.at[k], "rows", up)

    sides = ((has_xu, has_xd, x_up), (has_xd, has_xu, x_dn), (has_zu, has_zd, z_up), (has_zd, has_zu, z_dn))

    def start_sides(n):
        for sends, _, copy in sides:
            @pl.when(sends)
            def _():
                copy(n).start()

    def wait_side_sends(n):
        for sends, _, copy in sides:
            @pl.when(sends)
            def _():
                copy(n).wait_send()

    def wait_side_recvs(n):
        for _, gets, copy in sides:
            @pl.when(gets)
            def _():
                copy(n).wait_recv()

    def wait_y_sends(n, k):
        @pl.when(has_up)
        def _():
            y_up(n, k).wait_send()

        @pl.when(has_dn)
        def _():
            y_dn(n, k).wait_send()

    def wait_y_recvs(n, k):
        @pl.when(has_dn)
        def _():
            y_up(n, k).wait_recv()

        @pl.when(has_up)
        def _():
            y_dn(n, k).wait_recv()

    def each(count, body, start=0):
        def turn(i, carry):
            body(i)
            return carry
        lax.fori_loop(start, count, turn, 0)

    load_t = pltpu.make_async_copy(tr, out_t, load_sem.at[0])
    load_c = pltpu.make_async_copy(cr, out_c, load_sem.at[1])
    load_t.start()
    load_c.start()

    barrier = pltpu.get_barrier_semaphore()
    count = jnp.int32(0)
    for there, axis, index in ((has_up, "rows", up), (has_dn, "rows", dn), (has_xu, "cols", xu),
                               (has_xd, "cols", xd), (has_zu, "slabs", zu), (has_zd, "slabs", zd)):
        @pl.when(there)
        def _():
            pl.semaphore_signal(barrier, inc=1, device_id={axis: index}, device_id_type=MESH)
        count = count + there.astype(jnp.int32)
    pl.semaphore_wait(barrier, count)

    @pl.when(has_up)
    def _():
        each(CHUNKS, lambda k: y_up(0, k).start())

    @pl.when(has_dn)
    def _():
        each(CHUNKS, lambda k: y_dn(0, k).start())

    zeros = jnp.zeros((nz, nl), jnp.float32)

    @pl.when(jnp.logical_not(has_dn))
    def _():
        def clear(x):
            ylo[0, x] = zeros
            ylo[1, x] = zeros
            q[x] = zeros
        each(nx, clear)

    @pl.when(jnp.logical_not(has_up))
    def _():
        def clear(x):
            yhi[0, x] = zeros
            yhi[1, x] = zeros
        each(nx, clear)

    for there, ref in ((has_xd, xlo), (has_xu, xhi), (has_zd, zlo), (has_zu, zhi)):
        @pl.when(jnp.logical_not(there))
        def _():
            ref[...] = jnp.zeros_like(ref)

    load_t.wait()

    def stage(x):
        for y in range(ny):
            zsl[0, y, pl.ds(x, 1), :] = out_t[y, x, 0:1, :]
            zsh[0, y, pl.ds(x, 1), :] = out_t[y, x, nz - 1:nz, :]
    each(nx, stage)
    start_sides(0)
    load_c.wait()

    def update(n, x, y, left, right, values, low, high):
        now = n % 2
        v = values[y]
        total = left + right
        lower = jnp.where(first, zlo[now, y, pl.ds(x, 1), :], pltpu.roll(v, 1, 0))
        upper = jnp.where(final, zhi[now, y, pl.ds(x, 1), :], pltpu.roll(v, nz - 1, 0))
        total = total + (lower + upper)
        for other_y in (low, high):
            if other_y is not None:
                total = total + other_y
        return v * (0.6 - 0.2 * (out_c[y, x] * v)) + 0.1 * total

    def over_rows(k, body, n):
        src = fields[n % 2]
        now = n % 2
        low = jnp.maximum(k * width, 1)
        high = jnp.minimum((k + 1) * width, nx - 1)

        @pl.when(k == 0)
        def _():
            body(0, lambda y: xlo[now, y], lambda y: src[y, 1])

        each(high, lambda x: body(x, lambda y: src[y, x - 1], lambda y: src[y, x + 1]), low)

        @pl.when(k == CHUNKS - 1)
        def _():
            body(nx - 1, lambda y: src[y, nx - 2], lambda y: xhi[now, y])

    held_from = jnp.minimum(CHUNKS // 2 + 2 * row, CHUNKS)

    for n in range(STEPS - 1):
        src, dst = fields[n % 2], fields[(n + 1) % 2]
        now, later = n % 2, (n + 1) % 2
        if n >= 1:
            wait_side_sends(n - 1)
        wait_side_recvs(n)

        def one_row(x, left, right, n=n, src=src, dst=dst, now=now, later=later):
            values = [src[y, x] for y in range(ny)]
            for y in range(ny):
                below = values[y - 1] if y > 0 else ylo[now, x]
                above = values[y + 1] if y < ny - 1 else yhi[now, x]
                new = update(n, x, y, left(y), right(y), values, below, above)
                dst[y, x] = new
                zsl[later, y, pl.ds(x, 1), :] = new[0:1]
                zsh[later, y, pl.ds(x, 1), :] = new[nz - 1:nz]

        def one_chunk(k, n=n, one_row=one_row):
            wait_y_recvs(n, k)
            if n >= 1:
                wait_y_sends(n - 1, k)
            over_rows(k, one_row, n)
            goes_up = has_up if n + 1 < STEPS - 1 else jnp.logical_and(has_up, k < held_from)

            @pl.when(goes_up)
            def _():
                y_up(n + 1, k).start()

            @pl.when(has_dn)
            def _():
                y_dn(n + 1, k).start()

        each(CHUNKS, one_chunk)
        start_sides(n + 1)

    n = STEPS - 1
    src, dst = fields[n % 2], fields[(n + 1) % 2]
    wait_side_sends(n - 1)
    wait_side_recvs(n)

    def part_row(x, left, right):
        values = [src[y, x] for y in range(ny)]
        total = 0.1 * values[ny - 1] + inner * values[0]
        for y in range(ny):
            below = values[y - 1] if y > 0 else None
            above = values[y + 1] if y < ny - 1 else None
            new = update(n, x, y, left(y), right(y), values, below, above)
            dst[y, x] = new
            total = total + new
        g[x] = total

    def part_chunk(k):
        wait_y_sends(n - 1, k)
        over_rows(k, part_row, n)

        @pl.when(jnp.logical_not(has_dn))
        def _():
            q_up(k).start()
    each(CHUNKS, part_chunk)

    @pl.when(has_dn)
    def _():
        def pass_on(k):
            q_up(k).wait_recv()

            @pl.when(has_up)
            def _():
                def add(x):
                    g[x] = g[x] + q[x]
                each((k + 1) * width, add, k * width)
                q_up(k).start()
        each(CHUNKS, pass_on)

    @pl.when(has_up)
    def _():
        each(CHUNKS, lambda k: y_up(n, k).start(), held_from)

    scale = 1.0 / (ny * rows)

    def end_chunk(k):
        wait_y_recvs(n, k)

        def end_row(x):
            low = ylo[n % 2, x]
            sums = q[x] + inner * (src[0, x] - low)
            for y in range(ny):
                value = dst[y, x]
                if y == 0:
                    value = value + 0.1 * low
                if y == ny - 1:
                    value = value + 0.1 * yhi[n % 2, x]
                if y in (0, ny - 1):
                    dst[y, x] = value
                sums = sums + value
                out_c[y, x] = sums * scale
        each((k + 1) * width, end_row, k * width)
    each(CHUNKS, end_chunk)

    each(CHUNKS, lambda k: wait_y_sends(n, k))
    wait_side_sends(n)

    @pl.when(has_up)
    def _():
        each(CHUNKS, lambda k: q_up(k).wait_send())


def body(tracer, crowding):
    ny, nx, nz, nl = tracer.shape
    sizes = tuple(lax.axis_size(a) for a in ("rows", "cols", "slabs"))
    shape = jax.ShapeDtypeStruct(tracer.shape, jnp.float32)
    vmem = lambda *s: pltpu.VMEM(s, jnp.float32)
    dma = pltpu.SemaphoreType.DMA
    return pl.pallas_call(
        functools.partial(kernel, sizes),
        out_shape=(shape, shape),
        in_specs=[pl.BlockSpec(memory_space=pltpu.HBM)] * 2,
        out_specs=[pl.BlockSpec(memory_space=pltpu.VMEM)] * 2,
        scratch_shapes=[
            vmem(ny, nx, nz, nl),
            vmem(2, nx, nz, nl), vmem(2, nx, nz, nl),
            vmem(2, ny, nz, nl), vmem(2, ny, nz, nl),
            vmem(2, ny, nx, nl), vmem(2, ny, nx, nl),
            vmem(2, ny, nx, nl), vmem(2, ny, nx, nl),
            vmem(nx, nz, nl), vmem(nx, nz, nl),
            dma((2,)),
            dma((STEPS, CHUNKS)), dma((STEPS, CHUNKS)), dma((STEPS, CHUNKS)), dma((STEPS, CHUNKS)),
            dma((STEPS, 2)), dma((STEPS, 2)), dma((STEPS, 2)), dma((STEPS, 2)),
            dma((CHUNKS,)), dma((CHUNKS,)),
        ],
        compiler_params=pltpu.CompilerParams(
            collective_id=0, has_side_effects=True, vmem_limit_bytes=42 * 1024 * 1024),
        name="grid_steps",
    )(tracer, crowding)


def solution(mesh):
    placed = P("rows", "cols", "slabs", None)
    return jax.shard_map(body, mesh=mesh, in_specs=(placed, placed), out_specs=(placed, placed), check_vma=False)
```

time: 449 us -> 246 us (0.55)
  Pallas kernels: 0 us -> 233 us
  waiting for transfers between devices: 212 us -> 0 us
  other arithmetic: 124 us -> 0 us
  starting transfers between devices: 59.1 us -> 0 us
  local copies, waits for them, and re-layouts: 36.5 us -> 9.8 us
  between operations: 14.4 us -> 0.65 us
    pallas_call x0 -> x1, Pallas kernels: none -> 233 us  [body(): pl.pallas_call(functools.partial(kernel, sizes), out_shape=(shape, shape)...]
    ppermute x24 -> x0, waiting for transfers between devices: 128 us -> none  [the longest x12 113 us: extended(): lax.ppermute(last, axis, up)]
    add x4 -> x0, other arithmetic: 96.9 us -> none  [advance(): return middle + 0.1 * spread + 0.2 * middle * (1.0 - middle * crowding)]
    all_gather x1 -> x0, waiting for transfers between devices: 84.4 us -> none  [prefix(): everything = lax.all_gather(array, axis)]
    ppermute x24 -> x0, starting transfers between devices: 59 us -> none  [the longest x12 30.3 us: extended(): lax.ppermute(last, axis, up)]
    slice x13 -> x0, local copies, waits for them, and re-layouts: 24.3 us -> none  [the longest x11 18.5 us: extended(): last = lax.slice_in_dim(array, length - width, length, axis=dim)]
    select_n x4 -> x0, other arithmetic: 9.24 us -> none  [turn(): return jnp.where(reached, new, before)]
    div x1 -> x0, other arithmetic: 8.78 us -> none  [body(): column_sum = (here + below) / (tracer.shape[0] * lax.axis_size('rows'))]
  transfers between devices with their start and end apart: 25 -> 0, of which waited for: 14 -> 0; matrix products, arithmetic and copies ran while one was open for 5% -> 0% of each run, Pallas kernels for 0% -> 0%
where the time goes in v1:
time: 246 us; the launch traced here: 243 us
  Pallas kernels  233 us (95%)
  local copies, waits for them, and re-layouts  9.8 us (4%)
    pallas_call x1, Pallas kernels, body(): pl.pallas_call(functools.partial(kernel, sizes), out_shape=(shape, shape)...  233 us
    unnamed x4, local copies, waits for them, and re-layouts  9.8 us

profile of v1, /device:TPU:68, one launch (start us, length us, event | category | flops | bytes accessed | tf_op | source)
XLA Modules:
  0.0 243.3 jit_solution(14801483304791658864)
XLA Ops:
  0.6 232.8 %grid_steps.1 = (f32[4,64,64,128]{3,2,1,0:T(8,128)S(1)}, f32[4,64,64,128]{3,2,1,0:T(8,128)}) custom-call(f32[4,64,64,128]{3,2,1,0:T(8,128)} %tr.1, f32[4,64,64,128]{3,2,1,0:T(8,128)} %cr.1), custom_call_target="tpu_custom_call" | custom-call | tf_op jit(solution)/shard_map/grid_steps/pallas_call | solution.py:305
  233.4 0.0 copy-start
  233.5 4.3 %copy.6 = f32[4,64,64,128]{3,2,1,0:T(8,128)} copy(f32[4,64,64,128]{3,2,1,0:T(8,128)S(1)} %get-tuple-element.4) | data formatting | bytes 16777216
  237.7 2.1 copy-done
  239.9 3.4 %copy.7 = f32[4,64,64,128]{3,2,1,0:T(8,128)} copy(f32[4,64,64,128]{3,2,1,0:T(8,128)S(1)} %copy-done) | data formatting | bytes 16777216
Async XLA Ops:
  233.4 6.4 %copy-start = (f32[4,64,64,128]{3,2,1,0:T(8,128)S(1)}, f32[4,64,64,128]{3,2,1,0:T(8,128)}, u32[]{:S(2)}) copy-start(f32[4,64,64,128]{3,2,1,0:T(8,128)} %get-tuple-element.5) | copy-start | bytes 25165828

commit v2 on v1

--- a/solution.py
+++ b/solution.py
@@ -9,11 +9,13 @@
 
 STEPS = 4
 CHUNKS = 8
+PARTS = 16
+CUTS = (0, 5, 10, 16)
 MESH = pl.DeviceIdType.MESH
 
 
-def kernel(sizes, tr, cr, out_c, out_t, other, ylo, yhi, xlo, xhi, zlo, zhi, zsl, zsh, q, g,
-           load_sem, yu_s, yu_r, yd_s, yd_r, xs, xr, zs, zr, qs, qr):
+def kernel(sizes, tr, cr, out_c, out_t, other, ylo, yhi, xlo, xhi, zlo, zhi, zsl, zsh, qu, qd, g,
+           load_sem, yu_s, yu_r, yd_s, yd_r, xs, xr, zs, zr, qu_s, qu_r, qd_s, qd_r):
     rows, cols, slabs = sizes
     ny, nx, nz, nl = tr.shape
     width = nx // CHUNKS
@@ -34,7 +36,8 @@
             src_ref=src, dst_ref=dst, send_sem=send, recv_sem=recv,
             device_id={axis: index}, device_id_type=MESH)
 
-    up, dn = jnp.minimum(row + 1, rows - 1), jnp.maximum(row - 1, 0)
+    up, dn, back = jnp.minimum(row + 1, rows - 1), jnp.maximum(row - 1, 0), lax.rem(row + rows - 1, rows)
+    piece = nx // PARTS
     xu, xd = jnp.minimum(col + 1, cols - 1), jnp.maximum(col - 1, 0)
     zu, zd = jnp.minimum(slab + 1, slabs - 1), jnp.maximum(slab - 1, 0)
 
@@ -58,8 +61,14 @@
     def z_dn(n):
         return remote(zsl.at[n % 2], zhi.at[n % 2], zs.at[n, 1], zr.at[n, 1], "slabs", zd)
 
-    def q_up(k):
-        return remote(g.at[chunk(k)], q.at[chunk(k)], qs.at[k], qr.at[k], "rows", up)
+    def part(j):
+        return pl.ds(pl.multiple_of(j * piece, piece), piece)
+
+    def q_up(j):
+        return remote(g.at[part(j)], qu.at[part(j)], qu_s.at[j], qu_r.at[j], "rows", up)
+
+    def q_dn(j, src=g):
+        return remote(src.at[part(j)], qd.at[part(j)], qd_s.at[j], qd_r.at[j], "rows", back)
 
     sides = ((has_xu, has_xd, x_up), (has_xd, has_xu, x_dn), (has_zu, has_zd, z_up), (has_zd, has_zu, z_dn))
 
@@ -118,7 +127,12 @@
         def _():
             pl.semaphore_signal(barrier, inc=1, device_id={axis: index}, device_id_type=MESH)
         count = count + there.astype(jnp.int32)
-    pl.semaphore_wait(barrier, count)
+    ends = jnp.logical_or(row == 0, row == rows - 1)
+
+    @pl.when(ends)
+    def _():
+        pl.semaphore_signal(barrier, inc=1, device_id={"rows": rows - 1 - row}, device_id_type=MESH)
+    pl.semaphore_wait(barrier, count + ends.astype(jnp.int32))
 
     @pl.when(has_up)
     def _():
@@ -135,7 +149,6 @@
         def clear(x):
             ylo[0, x] = zeros
             ylo[1, x] = zeros
-            q[x] = zeros
         each(nx, clear)
 
     @pl.when(jnp.logical_not(has_up))
@@ -188,7 +201,7 @@
         def _():
             body(nx - 1, lambda y: src[y, nx - 2], lambda y: xhi[now, y])
 
-    held_from = jnp.minimum(CHUNKS // 2 + 2 * row, CHUNKS)
+    held_from = CHUNKS // 2
 
     for n in range(STEPS - 1):
         src, dst = fields[n % 2], fields[(n + 1) % 2]
@@ -218,7 +231,9 @@
             def _():
                 y_up(n + 1, k).start()
 
-            @pl.when(has_dn)
+            goes_dn = has_dn if n + 1 < STEPS - 1 else jnp.logical_and(has_dn, k < held_from)
+
+            @pl.when(goes_dn)
             def _():
                 y_dn(n + 1, k).start()
 
@@ -244,28 +259,93 @@
     def part_chunk(k):
         wait_y_sends(n - 1, k)
         over_rows(k, part_row, n)
-
-        @pl.when(jnp.logical_not(has_dn))
-        def _():
-            q_up(k).start()
     each(CHUNKS, part_chunk)
 
-    @pl.when(has_dn)
-    def _():
-        def pass_on(k):
-            q_up(k).wait_recv()
-
-            @pl.when(has_up)
-            def _():
-                def add(x):
-                    g[x] = g[x] + q[x]
-                each((k + 1) * width, add, k * width)
-                q_up(k).start()
-        each(CHUNKS, pass_on)
-
-    @pl.when(has_up)
-    def _():
+    def parts(s, body):
+        each(CUTS[s + 1], body, CUTS[s])
+
+    def over(j, body):
+        each((j + 1) * piece, body, j * piece)
+
+    def send(copy):
+        return lambda j: copy(j).start()
+
+    def rest_up():
         each(CHUNKS, lambda k: y_up(n, k).start(), held_from)
+
+    def rest_dn():
+        each(CHUNKS, lambda k: y_dn(n, k).start(), held_from)
+
+    @pl.when(row == 0)
+    def _():
+        parts(0, send(q_dn))
+        parts(2, send(q_up))
+        parts(1, send(q_up))
+        rest_up()
+
+        def around(j):
+            q_dn(j).wait_recv()
+
+            def add(x):
+                qd[x] = qd[x] + g[x]
+            over(j, add)
+            q_dn(j, qd).start()
+        parts(1, around)
+        parts(2, around)
+
+    @pl.when(row == 1)
+    def _():
+        parts(1, send(q_dn))
+        parts(0, send(q_up))
+
+        def both(j):
+            q_up(j).wait_recv()
+            q_dn(j).wait_recv()
+
+            def add(x):
+                own = g[x]
+                qd[x] = qd[x] + own
+                g[x] = qu[x] + own
+            over(j, add)
+            q_up(j).start()
+            q_dn(j, qd).start()
+        parts(2, both)
+        rest_up()
+        rest_dn()
+        each(CUTS[2], lambda j: q_up(j).wait_recv(), CUTS[1])
+        each(CUTS[1], lambda j: q_dn(j).wait_recv(), CUTS[0])
+
+    @pl.when(row == 2)
+    def _():
+        parts(2, send(q_dn))
+        parts(1, send(q_up))
+
+        def both(j):
+            q_up(j).wait_recv()
+
+            def add(x):
+                g[x] = qu[x] + g[x]
+            over(j, add)
+            q_up(j).start()
+            q_dn(j).wait_recv()
+            q_dn(j, qd).start()
+        parts(0, both)
+        rest_up()
+        rest_dn()
+        parts(1, lambda j: q_dn(j).wait_recv())
+        parts(2, lambda j: q_up(j).wait_recv())
+
+    @pl.when(row == 3)
+    def _():
+        def forward(j):
+            q_dn(j).wait_recv()
+            q_dn(j, qd).start()
+        parts(0, forward)
+        parts(1, forward)
+        rest_dn()
+        parts(0, lambda j: q_up(j).wait_recv())
+        parts(1, lambda j: q_up(j).wait_recv())
+        parts(2, lambda j: q_dn(j).wait_recv())
 
     scale = 1.0 / (ny * rows)
 
@@ -274,7 +354,11 @@
 
         def end_row(x):
             low = ylo[n % 2, x]
-            sums = q[x] + inner * (src[0, x] - low)
+            kind = (x >= CUTS[1] * piece).astype(jnp.int32) + (x >= CUTS[2] * piece).astype(jnp.int32)
+            use_u = jnp.logical_and(has_dn, kind != row - 1)
+            use_d = jnp.logical_and(has_dn, kind <= row - 1)
+            sums = lax.select(use_u, qu[x], zeros) + lax.select(use_d, qd[x], zeros)
+            sums = sums + inner * (src[0, x] - low)
             for y in range(ny):
                 value = dst[y, x]
                 if y == 0:
@@ -291,9 +375,22 @@
     each(CHUNKS, lambda k: wait_y_sends(n, k))
     wait_side_sends(n)
 
-    @pl.when(has_up)
-    def _():
-        each(CHUNKS, lambda k: q_up(k).wait_send())
+    for r in range(rows):
+        @pl.when(row == r)
+        def _():
+            for kind in range(3):
+                if r < rows - 1 and kind != r:
+                    parts(kind, lambda j: q_up(j).wait_send())
+                if kind not in {0: (), 1: (0,), 2: (1,), 3: (2,)}[r]:
+                    parts(kind, lambda j: q_dn(j).wait_send())
+
+
+def write(c_ref, t_ref, out_c, out_t, sem):
+    copies = [pltpu.make_async_copy(c_ref, out_c, sem.at[0]), pltpu.make_async_copy(t_ref, out_t, sem.at[1])]
+    for copy in copies:
+        copy.start()
+    for copy in copies:
+        copy.wait()
 
 
 def body(tracer, crowding):
@@ -302,7 +399,7 @@
     shape = jax.ShapeDtypeStruct(tracer.shape, jnp.float32)
     vmem = lambda *s: pltpu.VMEM(s, jnp.float32)
     dma = pltpu.SemaphoreType.DMA
-    return pl.pallas_call(
+    sums, field = pl.pallas_call(
         functools.partial(kernel, sizes),
         out_shape=(shape, shape),
         in_specs=[pl.BlockSpec(memory_space=pltpu.HBM)] * 2,
@@ -313,16 +410,25 @@
             vmem(2, ny, nz, nl), vmem(2, ny, nz, nl),
             vmem(2, ny, nx, nl), vmem(2, ny, nx, nl),
             vmem(2, ny, nx, nl), vmem(2, ny, nx, nl),
-            vmem(nx, nz, nl), vmem(nx, nz, nl),
+            vmem(nx, nz, nl), vmem(nx, nz, nl), vmem(nx, nz, nl),
             dma((2,)),
             dma((STEPS, CHUNKS)), dma((STEPS, CHUNKS)), dma((STEPS, CHUNKS)), dma((STEPS, CHUNKS)),
             dma((STEPS, 2)), dma((STEPS, 2)), dma((STEPS, 2)), dma((STEPS, 2)),
-            dma((CHUNKS,)), dma((CHUNKS,)),
+            dma((PARTS,)), dma((PARTS,)), dma((PARTS,)), dma((PARTS,)),
         ],
         compiler_params=pltpu.CompilerParams(
-            collective_id=0, has_side_effects=True, vmem_limit_bytes=42 * 1024 * 1024),
+            collective_id=0, has_side_effects=True, vmem_limit_bytes=30 * 1024 * 1024),
         name="grid_steps",
     )(tracer, crowding)
+    return pl.pallas_call(
+        write,
+        out_shape=(shape, shape),
+        in_specs=[pl.BlockSpec(memory_space=pltpu.VMEM)] * 2,
+        out_specs=[pl.BlockSpec(memory_space=pltpu.HBM)] * 2,
+        scratch_shapes=[dma((2,))],
+        compiler_params=pltpu.CompilerParams(vmem_limit_bytes=1024 * 1024),
+        name="write_out",
+    )(sums, field)
 
 
 def solution(mesh):

time: 246 us -> 226 us (0.919)
  Pallas kernels: 233 us -> 222 us
  local copies, waits for them, and re-layouts: 9.8 us -> 0 us
    pallas_call x1, Pallas kernels: 233 us -> 216 us  [body(): pl.pallas_call(functools.partial(kernel, sizes), out_shape=(shape, shape)...]
    unnamed x4 -> x0, local copies, waits for them, and re-layouts: 9.8 us -> none
    pallas_call x0 -> x1, Pallas kernels: none -> 6.18 us  [body(): pl.pallas_call(write, out_shape=(shape, shape), in_specs=[pl.BlockSpec(me...]
where the time goes in v2:
time: 226 us; the launch traced here: 223 us
  Pallas kernels  222 us (98%)
    pallas_call x1, Pallas kernels, body(): pl.pallas_call(functools.partial(kernel, sizes), out_shape=(shape, shape)...  216 us
    pallas_call x1, Pallas kernels, body(): pl.pallas_call(write, out_shape=(shape, shape), in_specs=[pl.BlockSpec(me...  6.18 us

profile of v2, /device:TPU:68, one launch (start us, length us, event | category | flops | bytes accessed | tf_op | source)
XLA Modules:
  0.0 222.9 jit_solution(8288666735482832596)
XLA Ops:
  0.6 216.1 %grid_steps.1 = (f32[4,64,64,128]{3,2,1,0:T(8,128)S(1)}, f32[4,64,64,128]{3,2,1,0:T(8,128)S(1)}) custom-call(f32[4,64,64,128]{3,2,1,0:T(8,128)} %tr.1, f32[4,64,64,128]{3,2,1,0:T(8,128)} %cr.1), custom_call_target="tpu_custom_call" | custom-call | tf_op jit(solution)/shard_map/grid_steps/pallas_call | solution.py:402
  216.8 6.2 %write_out.1 = (f32[4,64,64,128]{3,2,1,0:T(8,128)}, f32[4,64,64,128]{3,2,1,0:T(8,128)}) custom-call(f32[4,64,64,128]{3,2,1,0:T(8,128)S(1)} %get-tuple-element.4.c_ref, f32[4,64,64,128]{3,2,1,0:T(8,128)S(1)} %get-tuple-element.5.t_ref), custom_call_target="tpu_custom_call" | custom-call | tf_op jit(solution)/shard_map/write_out/pallas_call | solution.py:423

commit v3 on v2

--- a/solution.py
+++ b/solution.py
@@ -8,10 +8,22 @@
 from jax.sharding import PartitionSpec as P
 
 STEPS = 4
-CHUNKS = 8
-PARTS = 16
-CUTS = (0, 5, 10, 16)
+CHUNKS = 4
+HELD = 3
+WRITES = 4
+SHARES = (22, 21, 21)
 MESH = pl.DeviceIdType.MESH
+
+
+def column_sets(nx):
+    counts = [share * nx // sum(SHARES) for share in SHARES]
+    counts[2] = nx - counts[0] - counts[1]
+    sets, start, base = [], 0, 0
+    for count in counts:
+        piece = next(p for p in (11, 7, 6, 5, 4, 3, 2, 1) if count % p == 0)
+        sets.append((start, count // piece, piece, base))
+        start, base = start + count, base + count // piece
+    return sets
 
 
 def kernel(sizes, tr, cr, out_c, out_t, other, ylo, yhi, xlo, xhi, zlo, zhi, zsl, zsh, qu, qd, g,
@@ -37,17 +49,15 @@
             device_id={axis: index}, device_id_type=MESH)
 
     up, dn, back = jnp.minimum(row + 1, rows - 1), jnp.maximum(row - 1, 0), lax.rem(row + rows - 1, rows)
-    piece = nx // PARTS
+    sets = column_sets(nx)
     xu, xd = jnp.minimum(col + 1, cols - 1), jnp.maximum(col - 1, 0)
     zu, zd = jnp.minimum(slab + 1, slabs - 1), jnp.maximum(slab - 1, 0)
 
     def y_up(n, k):
-        src = tr if n == 0 else fields[n % 2]
-        return remote(src.at[ny - 1, chunk(k)], ylo.at[n % 2, chunk(k)], yu_s.at[n, k], yu_r.at[n, k], "rows", up)
+        return remote(fields[n % 2].at[ny - 1, chunk(k)], ylo.at[n % 2, chunk(k)], yu_s.at[n, k], yu_r.at[n, k], "rows", up)
 
     def y_dn(n, k):
-        src = tr if n == 0 else fields[n % 2]
-        return remote(src.at[0, chunk(k)], yhi.at[n % 2, chunk(k)], yd_s.at[n, k], yd_r.at[n, k], "rows", dn)
+        return remote(fields[n % 2].at[0, chunk(k)], yhi.at[n % 2, chunk(k)], yd_s.at[n, k], yd_r.at[n, k], "rows", dn)
 
     def x_up(n):
         return remote(fields[n % 2].at[:, nx - 1], xlo.at[n % 2], xs.at[n, 0], xr.at[n, 0], "cols", xu)
@@ -61,14 +71,17 @@
     def z_dn(n):
         return remote(zsl.at[n % 2], zhi.at[n % 2], zs.at[n, 1], zr.at[n, 1], "slabs", zd)
 
-    def part(j):
-        return pl.ds(pl.multiple_of(j * piece, piece), piece)
-
-    def q_up(j):
-        return remote(g.at[part(j)], qu.at[part(j)], qu_s.at[j], qu_r.at[j], "rows", up)
-
-    def q_dn(j, src=g):
-        return remote(src.at[part(j)], qd.at[part(j)], qd_s.at[j], qd_r.at[j], "rows", back)
+    def part(kind, i):
+        start, _, piece, _ = sets[kind]
+        return pl.ds(start + i * piece, piece)
+
+    def q_up(kind, i):
+        j = sets[kind][3] + i
+        return remote(g.at[part(kind, i)], qu.at[part(kind, i)], qu_s.at[j], qu_r.at[j], "rows", up)
+
+    def q_dn(kind, i, src=g):
+        j = sets[kind][3] + i
+        return remote(src.at[part(kind, i)], qd.at[part(kind, i)], qd_s.at[j], qd_r.at[j], "rows", back)
 
     sides = ((has_xu, has_xd, x_up), (has_xd, has_xu, x_dn), (has_zu, has_zd, z_up), (has_zd, has_zu, z_dn))
 
@@ -114,8 +127,12 @@
             return carry
         lax.fori_loop(start, count, turn, 0)
 
-    load_t = pltpu.make_async_copy(tr, out_t, load_sem.at[0])
-    load_c = pltpu.make_async_copy(cr, out_c, load_sem.at[1])
+    inside = pl.ds(1, ny - 2)
+    load_ends = [pltpu.make_async_copy(tr.at[y], out_t.at[y], load_sem.at[i]) for i, y in enumerate((0, ny - 1))]
+    load_t = pltpu.make_async_copy(tr.at[inside], out_t.at[inside], load_sem.at[2])
+    load_c = pltpu.make_async_copy(cr, out_c, load_sem.at[3])
+    for load in load_ends:
+        load.start()
     load_t.start()
     load_c.start()
 
@@ -133,6 +150,9 @@
     def _():
         pl.semaphore_signal(barrier, inc=1, device_id={"rows": rows - 1 - row}, device_id_type=MESH)
     pl.semaphore_wait(barrier, count + ends.astype(jnp.int32))
+
+    for load in load_ends:
+        load.wait()
 
     @pl.when(has_up)
     def _():
@@ -201,7 +221,7 @@
         def _():
             body(nx - 1, lambda y: src[y, nx - 2], lambda y: xhi[now, y])
 
-    held_from = CHUNKS // 2
+    held_from = HELD
 
     for n in range(STEPS - 1):
         src, dst = fields[n % 2], fields[(n + 1) % 2]
@@ -261,14 +281,15 @@
         over_rows(k, part_row, n)
     each(CHUNKS, part_chunk)
 
-    def parts(s, body):
-        each(CUTS[s + 1], body, CUTS[s])
-
-    def over(j, body):
-        each((j + 1) * piece, body, j * piece)
+    def parts(kind, body):
+        each(sets[kind][1], lambda i: body(kind, i))
+
+    def over(kind, i, body):
+        start, _, piece, _ = sets[kind]
+        each(start + (i + 1) * piece, body, start + i * piece)
 
     def send(copy):
-        return lambda j: copy(j).start()
+        return lambda kind, i: copy(kind, i).start()
 
     def rest_up():
         each(CHUNKS, lambda k: y_up(n, k).start(), held_from)
@@ -283,13 +304,13 @@
         parts(1, send(q_up))
         rest_up()
 
-        def around(j):
-            q_dn(j).wait_recv()
+        def around(kind, i):
+            q_dn(kind, i).wait_recv()
 
             def add(x):
                 qd[x] = qd[x] + g[x]
-            over(j, add)
-            q_dn(j, qd).start()
+            over(kind, i, add)
+            q_dn(kind, i, qd).start()
         parts(1, around)
         parts(2, around)
 
@@ -298,54 +319,54 @@
         parts(1, send(q_dn))
         parts(0, send(q_up))
 
-        def both(j):
-            q_up(j).wait_recv()
-            q_dn(j).wait_recv()
+        def both(kind, i):
+            q_up(kind, i).wait_recv()
+            q_dn(kind, i).wait_recv()
 
             def add(x):
                 own = g[x]
                 qd[x] = qd[x] + own
                 g[x] = qu[x] + own
-            over(j, add)
-            q_up(j).start()
-            q_dn(j, qd).start()
+            over(kind, i, add)
+            q_up(kind, i).start()
+            q_dn(kind, i, qd).start()
         parts(2, both)
         rest_up()
         rest_dn()
-        each(CUTS[2], lambda j: q_up(j).wait_recv(), CUTS[1])
-        each(CUTS[1], lambda j: q_dn(j).wait_recv(), CUTS[0])
+        parts(1, lambda kind, i: q_up(kind, i).wait_recv())
+        parts(0, lambda kind, i: q_dn(kind, i).wait_recv())
 
     @pl.when(row == 2)
     def _():
         parts(2, send(q_dn))
         parts(1, send(q_up))
 
-        def both(j):
-            q_up(j).wait_recv()
+        def both(kind, i):
+            q_up(kind, i).wait_recv()
 
             def add(x):
                 g[x] = qu[x] + g[x]
-            over(j, add)
-            q_up(j).start()
-            q_dn(j).wait_recv()
-            q_dn(j, qd).start()
+            over(kind, i, add)
+            q_up(kind, i).start()
+            q_dn(kind, i).wait_recv()
+            q_dn(kind, i, qd).start()
         parts(0, both)
         rest_up()
         rest_dn()
-        parts(1, lambda j: q_dn(j).wait_recv())
-        parts(2, lambda j: q_up(j).wait_recv())
+        parts(1, lambda kind, i: q_dn(kind, i).wait_recv())
+        parts(2, lambda kind, i: q_up(kind, i).wait_recv())
 
     @pl.when(row == 3)
     def _():
-        def forward(j):
-            q_dn(j).wait_recv()
-            q_dn(j, qd).start()
+        def forward(kind, i):
+            q_dn(kind, i).wait_recv()
+            q_dn(kind, i, qd).start()
         parts(0, forward)
         parts(1, forward)
         rest_dn()
-        parts(0, lambda j: q_up(j).wait_recv())
-        parts(1, lambda j: q_up(j).wait_recv())
-        parts(2, lambda j: q_dn(j).wait_recv())
+        parts(0, lambda kind, i: q_up(kind, i).wait_recv())
+        parts(1, lambda kind, i: q_up(kind, i).wait_recv())
+        parts(2, lambda kind, i: q_dn(kind, i).wait_recv())
 
     scale = 1.0 / (ny * rows)
 
@@ -354,7 +375,7 @@
 
         def end_row(x):
             low = ylo[n % 2, x]
-            kind = (x >= CUTS[1] * piece).astype(jnp.int32) + (x >= CUTS[2] * piece).astype(jnp.int32)
+            kind = (x >= sets[1][0]).astype(jnp.int32) + (x >= sets[2][0]).astype(jnp.int32)
             use_u = jnp.logical_and(has_dn, kind != row - 1)
             use_d = jnp.logical_and(has_dn, kind <= row - 1)
             sums = lax.select(use_u, qu[x], zeros) + lax.select(use_d, qd[x], zeros)
@@ -380,13 +401,18 @@
         def _():
             for kind in range(3):
                 if r < rows - 1 and kind != r:
-                    parts(kind, lambda j: q_up(j).wait_send())
+                    parts(kind, lambda kind, i: q_up(kind, i).wait_send())
                 if kind not in {0: (), 1: (0,), 2: (1,), 3: (2,)}[r]:
-                    parts(kind, lambda j: q_dn(j).wait_send())
+                    parts(kind, lambda kind, i: q_dn(kind, i).wait_send())
 
 
 def write(c_ref, t_ref, out_c, out_t, sem):
-    copies = [pltpu.make_async_copy(c_ref, out_c, sem.at[0]), pltpu.make_async_copy(t_ref, out_t, sem.at[1])]
+    copies = []
+    for i, (src, dst) in enumerate(((c_ref, out_c), (t_ref, out_t))):
+        for j in range(WRITES):
+            width = src.shape[1] // WRITES
+            at = (slice(None), pl.ds(j * width, width)) if WRITES > src.shape[0] else (pl.ds(j * (src.shape[0] // WRITES), src.shape[0] // WRITES),)
+            copies.append(pltpu.make_async_copy(src.at[at], dst.at[at], sem.at[i, j]))
     for copy in copies:
         copy.start()
     for copy in copies:
@@ -399,6 +425,7 @@
     shape = jax.ShapeDtypeStruct(tracer.shape, jnp.float32)
     vmem = lambda *s: pltpu.VMEM(s, jnp.float32)
     dma = pltpu.SemaphoreType.DMA
+    parts = sum(count for _, count, _, _ in column_sets(nx))
     sums, field = pl.pallas_call(
         functools.partial(kernel, sizes),
         out_shape=(shape, shape),
@@ -411,10 +438,10 @@
             vmem(2, ny, nx, nl), vmem(2, ny, nx, nl),
             vmem(2, ny, nx, nl), vmem(2, ny, nx, nl),
             vmem(nx, nz, nl), vmem(nx, nz, nl), vmem(nx, nz, nl),
-            dma((2,)),
+            dma((4,)),
             dma((STEPS, CHUNKS)), dma((STEPS, CHUNKS)), dma((STEPS, CHUNKS)), dma((STEPS, CHUNKS)),
             dma((STEPS, 2)), dma((STEPS, 2)), dma((STEPS, 2)), dma((STEPS, 2)),
-            dma((PARTS,)), dma((PARTS,)), dma((PARTS,)), dma((PARTS,)),
+            dma((parts,)), dma((parts,)), dma((parts,)), dma((parts,)),
         ],
         compiler_params=pltpu.CompilerParams(
             collective_id=0, has_side_effects=True, vmem_limit_bytes=30 * 1024 * 1024),
@@ -425,7 +452,7 @@
         out_shape=(shape, shape),
         in_specs=[pl.BlockSpec(memory_space=pltpu.VMEM)] * 2,
         out_specs=[pl.BlockSpec(memory_space=pltpu.HBM)] * 2,
-        scratch_shapes=[dma((2,))],
+        scratch_shapes=[dma((2, WRITES))],
         compiler_params=pltpu.CompilerParams(vmem_limit_bytes=1024 * 1024),
         name="write_out",
     )(sums, field)

time: 226 us -> 224 us (level)
  no operation moved by 1% of the time
where the time goes in v3:
time: 224 us; the launch traced here: 223 us
  Pallas kernels  222 us (99%)
    pallas_call x1, Pallas kernels, body(): pl.pallas_call(functools.partial(kernel, sizes), out_shape=(shape, shape)...  216 us
    pallas_call x1, Pallas kernels, body(): pl.pallas_call(write, out_shape=(shape, shape), in_specs=[pl.BlockSpec(me...  5.93 us

profile of v3, /device:TPU:68, one launch (start us, length us, event | category | flops | bytes accessed | tf_op | source)
XLA Modules:
  0.0 222.9 jit_solution(10813188432930237031)
XLA Ops:
  0.6 216.3 %grid_steps.1 = (f32[4,64,64,128]{3,2,1,0:T(8,128)S(1)}, f32[4,64,64,128]{3,2,1,0:T(8,128)S(1)}) custom-call(f32[4,64,64,128]{3,2,1,0:T(8,128)} %tr.1, f32[4,64,64,128]{3,2,1,0:T(8,128)} %cr.1), custom_call_target="tpu_custom_call" | custom-call | tf_op jit(solution)/shard_map/grid_steps/pallas_call | solution.py:429
  216.9 5.9 %write_out.1 = (f32[4,64,64,128]{3,2,1,0:T(8,128)}, f32[4,64,64,128]{3,2,1,0:T(8,128)}) custom-call(f32[4,64,64,128]{3,2,1,0:T(8,128)S(1)} %get-tuple-element.4.c_ref, f32[4,64,64,128]{3,2,1,0:T(8,128)S(1)} %get-tuple-element.5.t_ref), custom_call_target="tpu_custom_call" | custom-call | tf_op jit(solution)/shard_map/write_out/pallas_call | solution.py:450

commit v4 on v3

--- a/solution.py
+++ b/solution.py
@@ -8,8 +8,9 @@
 from jax.sharding import PartitionSpec as P
 
 STEPS = 4
-CHUNKS = 4
-HELD = 3
+CHUNKS = 2
+HELD = 1
+TAILS = 4
 WRITES = 4
 SHARES = (22, 21, 21)
 MESH = pl.DeviceIdType.MESH
@@ -27,7 +28,7 @@
 
 
 def kernel(sizes, tr, cr, out_c, out_t, other, ylo, yhi, xlo, xhi, zlo, zhi, zsl, zsh, qu, qd, g,
-           load_sem, yu_s, yu_r, yd_s, yd_r, xs, xr, zs, zr, qu_s, qu_r, qd_s, qd_r):
+           load_sem, yu_s, yu_r, yd_s, yd_r, xs, xr, zs, zr, qu_s, qu_r, qd_s, qd_r, tail_s, tail_r):
     rows, cols, slabs = sizes
     ny, nx, nz, nl = tr.shape
     width = nx // CHUNKS
@@ -40,6 +41,16 @@
     final = lax.broadcasted_iota(jnp.int32, (nz, nl), 0) == nz - 1
     inner = jnp.where(has_dn, jnp.float32(0.1), jnp.float32(0.0))
 
+    early = slab < slabs // 2
+    below_middle, above_middle = col == cols // 2 - 1, col == cols // 2
+    late_xu = jnp.logical_and(below_middle, early)
+    late_xd = jnp.logical_and(above_middle, jnp.logical_not(early))
+    quiet_xu = jnp.logical_and(below_middle, jnp.logical_not(early))
+    quiet_xd = jnp.logical_and(above_middle, early)
+
+    def both_but(a, b):
+        return jnp.logical_and(a, jnp.logical_not(b))
+
     def chunk(k):
         return pl.ds(pl.multiple_of(k * width, width), width)
 
@@ -59,6 +70,19 @@
     def y_dn(n, k):
         return remote(fields[n % 2].at[0, chunk(k)], yhi.at[n % 2, chunk(k)], yd_s.at[n, k], yd_r.at[n, k], "rows", dn)
 
+    def tail(j):
+        start = HELD * width
+        size = (nx - start) // TAILS
+        return pl.ds(start + j * size, size)
+
+    def tail_up(j):
+        here = fields[(STEPS - 1) % 2].at[ny - 1, tail(j)]
+        return remote(here, ylo.at[(STEPS - 1) % 2, tail(j)], tail_s.at[0, j], tail_r.at[0, j], "rows", up)
+
+    def tail_dn(j):
+        here = fields[(STEPS - 1) % 2].at[0, tail(j)]
+        return remote(here, yhi.at[(STEPS - 1) % 2, tail(j)], tail_s.at[1, j], tail_r.at[1, j], "rows", dn)
+
     def x_up(n):
         return remote(fields[n % 2].at[:, nx - 1], xlo.at[n % 2], xs.at[n, 0], xr.at[n, 0], "cols", xu)
 
@@ -87,6 +111,11 @@
 
     def start_sides(n):
         for sends, _, copy in sides:
+            if n == 0 and copy is x_up:
+                sends = both_but(sends, late_xu)
+            if n == 0 and copy is x_dn:
+                sends = both_but(sends, late_xd)
+
             @pl.when(sends)
             def _():
                 copy(n).start()
@@ -138,12 +167,15 @@
 
     barrier = pltpu.get_barrier_semaphore()
     count = jnp.int32(0)
-    for there, axis, index in ((has_up, "rows", up), (has_dn, "rows", dn), (has_xu, "cols", xu),
-                               (has_xd, "cols", xd), (has_zu, "slabs", zu), (has_zd, "slabs", zd)):
-        @pl.when(there)
+    for says, hears, axis, index in (
+            (has_up, has_up, "rows", up), (has_dn, has_dn, "rows", dn),
+            (both_but(has_xu, quiet_xu), both_but(has_xu, late_xu), "cols", xu),
+            (both_but(has_xd, quiet_xd), both_but(has_xd, late_xd), "cols", xd),
+            (has_zu, has_zu, "slabs", zu), (has_zd, has_zd, "slabs", zd)):
+        @pl.when(says)
         def _():
             pl.semaphore_signal(barrier, inc=1, device_id={axis: index}, device_id_type=MESH)
-        count = count + there.astype(jnp.int32)
+        count = count + hears.astype(jnp.int32)
     ends = jnp.logical_or(row == 0, row == rows - 1)
 
     @pl.when(ends)
@@ -221,14 +253,17 @@
         def _():
             body(nx - 1, lambda y: src[y, nx - 2], lambda y: xhi[now, y])
 
-    held_from = HELD
-
     for n in range(STEPS - 1):
         src, dst = fields[n % 2], fields[(n + 1) % 2]
         now, later = n % 2, (n + 1) % 2
         if n >= 1:
             wait_side_sends(n - 1)
         wait_side_recvs(n)
+        if n == 0:
+            for late, copy in ((late_xu, x_up), (late_xd, x_dn)):
+                @pl.when(late)
+                def _():
+                    copy(0).start()
 
         def one_row(x, left, right, n=n, src=src, dst=dst, now=now, later=later):
             values = [src[y, x] for y in range(ny)]
@@ -245,13 +280,13 @@
             if n >= 1:
                 wait_y_sends(n - 1, k)
             over_rows(k, one_row, n)
-            goes_up = has_up if n + 1 < STEPS - 1 else jnp.logical_and(has_up, k < held_from)
+            goes_up = has_up if n + 1 < STEPS - 1 else jnp.logical_and(has_up, k < HELD)
 
             @pl.when(goes_up)
             def _():
                 y_up(n + 1, k).start()
 
-            goes_dn = has_dn if n + 1 < STEPS - 1 else jnp.logical_and(has_dn, k < held_from)
+            goes_dn = has_dn if n + 1 < STEPS - 1 else jnp.logical_and(has_dn, k < HELD)
 
             @pl.when(goes_dn)
             def _():
@@ -292,10 +327,10 @@
         return lambda kind, i: copy(kind, i).start()
 
     def rest_up():
-        each(CHUNKS, lambda k: y_up(n, k).start(), held_from)
+        each(TAILS, lambda j: tail_up(j).start())
 
     def rest_dn():
-        each(CHUNKS, lambda k: y_dn(n, k).start(), held_from)
+        each(TAILS, lambda j: tail_dn(j).start())
 
     @pl.when(row == 0)
     def _():
@@ -370,30 +405,50 @@
 
     scale = 1.0 / (ny * rows)
 
+    def end_row(x):
+        low = ylo[n % 2, x]
+        kind = (x >= sets[1][0]).astype(jnp.int32) + (x >= sets[2][0]).astype(jnp.int32)
+        use_u = jnp.logical_and(has_dn, kind != row - 1)
+        use_d = jnp.logical_and(has_dn, kind <= row - 1)
+        sums = lax.select(use_u, qu[x], zeros) + lax.select(use_d, qd[x], zeros)
+        sums = sums + inner * (src[0, x] - low)
+        for y in range(ny):
+            value = dst[y, x]
+            if y == 0:
+                value = value + 0.1 * low
+            if y == ny - 1:
+                value = value + 0.1 * yhi[n % 2, x]
+            if y in (0, ny - 1):
+                dst[y, x] = value
+            sums = sums + value
+            out_c[y, x] = sums * scale
+
     def end_chunk(k):
         wait_y_recvs(n, k)
-
-        def end_row(x):
-            low = ylo[n % 2, x]
-            kind = (x >= sets[1][0]).astype(jnp.int32) + (x >= sets[2][0]).astype(jnp.int32)
-            use_u = jnp.logical_and(has_dn, kind != row - 1)
-            use_d = jnp.logical_and(has_dn, kind <= row - 1)
-            sums = lax.select(use_u, qu[x], zeros) + lax.select(use_d, qd[x], zeros)
-            sums = sums + inner * (src[0, x] - low)
-            for y in range(ny):
-                value = dst[y, x]
-                if y == 0:
-                    value = value + 0.1 * low
-                if y == ny - 1:
-                    value = value + 0.1 * yhi[n % 2, x]
-                if y in (0, ny - 1):
-                    dst[y, x] = value
-                sums = sums + value
-                out_c[y, x] = sums * scale
         each((k + 1) * width, end_row, k * width)
-    each(CHUNKS, end_chunk)
-
-    each(CHUNKS, lambda k: wait_y_sends(n, k))
+    each(HELD, end_chunk)
+
+    def end_tail(j):
+        @pl.when(has_dn)
+        def _():
+            tail_up(j).wait_recv()
+
+        @pl.when(has_up)
+        def _():
+            tail_dn(j).wait_recv()
+        size = (nx - HELD * width) // TAILS
+        each(HELD * width + (j + 1) * size, end_row, HELD * width + j * size)
+    each(TAILS, end_tail)
+
+    each(HELD, lambda k: wait_y_sends(n, k))
+
+    @pl.when(has_up)
+    def _():
+        each(TAILS, lambda j: tail_up(j).wait_send())
+
+    @pl.when(has_dn)
+    def _():
+        each(TAILS, lambda j: tail_dn(j).wait_send())
     wait_side_sends(n)
 
     for r in range(rows):
@@ -442,6 +497,7 @@
             dma((STEPS, CHUNKS)), dma((STEPS, CHUNKS)), dma((STEPS, CHUNKS)), dma((STEPS, CHUNKS)),
             dma((STEPS, 2)), dma((STEPS, 2)), dma((STEPS, 2)), dma((STEPS, 2)),
             dma((parts,)), dma((parts,)), dma((parts,)), dma((parts,)),
+            dma((2, TAILS)), dma((2, TAILS)),
         ],
         compiler_params=pltpu.CompilerParams(
             collective_id=0, has_side_effects=True, vmem_limit_bytes=30 * 1024 * 1024),

time: 224 us -> 223 us (level)
  no operation moved by 1% of the time
where the time goes in v4:
time: 223 us
  Pallas kernels  223 us (100%)
    pallas_call x1, Pallas kernels, body(): pl.pallas_call(functools.partial(kernel, sizes), out_shape=(shape, shape)...  217 us
    pallas_call x1, Pallas kernels, body(): pl.pallas_call(write, out_shape=(shape, shape), in_specs=[pl.BlockSpec(me...  5.93 us

profile of v4, /device:TPU:68, one launch (start us, length us, event | category | flops | bytes accessed | tf_op | source)
XLA Modules:
  0.0 223.2 jit_solution(4764613386008163302)
XLA Ops:
  0.6 216.7 %grid_steps.1 = (f32[4,64,64,128]{3,2,1,0:T(8,128)S(1)}, f32[4,64,64,128]{3,2,1,0:T(8,128)S(1)}) custom-call(f32[4,64,64,128]{3,2,1,0:T(8,128)} %tr.1, f32[4,64,64,128]{3,2,1,0:T(8,128)} %cr.1), custom_call_target="tpu_custom_call" | custom-call | tf_op jit(solution)/shard_map/grid_steps/pallas_call | solution.py:484
  217.3 5.9 %write_out.1 = (f32[4,64,64,128]{3,2,1,0:T(8,128)}, f32[4,64,64,128]{3,2,1,0:T(8,128)}) custom-call(f32[4,64,64,128]{3,2,1,0:T(8,128)S(1)} %get-tuple-element.4.c_ref, f32[4,64,64,128]{3,2,1,0:T(8,128)S(1)} %get-tuple-element.5.t_ref), custom_call_target="tpu_custom_call" | custom-call | tf_op jit(solution)/shard_map/write_out/pallas_call | solution.py:506

commit v5 on v4

--- a/solution.py
+++ b/solution.py
@@ -12,12 +12,12 @@
 HELD = 1
 TAILS = 4
 WRITES = 4
-SHARES = (22, 21, 21)
+SHARES = ((21, 22, 21), (22, 21, 21))
 MESH = pl.DeviceIdType.MESH
 
 
-def column_sets(nx):
-    counts = [share * nx // sum(SHARES) for share in SHARES]
+def column_sets(nx, shares):
+    counts = [share * nx // sum(shares) for share in shares]
     counts[2] = nx - counts[0] - counts[1]
     sets, start, base = [], 0, 0
     for count in counts:
@@ -60,7 +60,9 @@
             device_id={axis: index}, device_id_type=MESH)
 
     up, dn, back = jnp.minimum(row + 1, rows - 1), jnp.maximum(row - 1, 0), lax.rem(row + rows - 1, rows)
-    sets = column_sets(nx)
+    choices = [column_sets(nx, shares) for shares in SHARES]
+    sets = list(choices[0])
+    core = lax.rem(slab, len(choices))
     xu, xd = jnp.minimum(col + 1, cols - 1), jnp.maximum(col - 1, 0)
     zu, zd = jnp.minimum(slab + 1, slabs - 1), jnp.maximum(slab - 1, 0)
 
@@ -332,82 +334,87 @@
     def rest_dn():
         each(TAILS, lambda j: tail_dn(j).start())
 
-    @pl.when(row == 0)
-    def _():
-        parts(0, send(q_dn))
-        parts(2, send(q_up))
-        parts(1, send(q_up))
-        rest_up()
-
-        def around(kind, i):
-            q_dn(kind, i).wait_recv()
-
-            def add(x):
-                qd[x] = qd[x] + g[x]
-            over(kind, i, add)
-            q_dn(kind, i, qd).start()
-        parts(1, around)
-        parts(2, around)
-
-    @pl.when(row == 1)
-    def _():
-        parts(1, send(q_dn))
-        parts(0, send(q_up))
-
-        def both(kind, i):
-            q_up(kind, i).wait_recv()
-            q_dn(kind, i).wait_recv()
-
-            def add(x):
-                own = g[x]
-                qd[x] = qd[x] + own
-                g[x] = qu[x] + own
-            over(kind, i, add)
-            q_up(kind, i).start()
-            q_dn(kind, i, qd).start()
-        parts(2, both)
-        rest_up()
-        rest_dn()
-        parts(1, lambda kind, i: q_up(kind, i).wait_recv())
-        parts(0, lambda kind, i: q_dn(kind, i).wait_recv())
-
-    @pl.when(row == 2)
-    def _():
-        parts(2, send(q_dn))
-        parts(1, send(q_up))
-
-        def both(kind, i):
-            q_up(kind, i).wait_recv()
-
-            def add(x):
-                g[x] = qu[x] + g[x]
-            over(kind, i, add)
-            q_up(kind, i).start()
-            q_dn(kind, i).wait_recv()
-            q_dn(kind, i, qd).start()
-        parts(0, both)
-        rest_up()
-        rest_dn()
-        parts(1, lambda kind, i: q_dn(kind, i).wait_recv())
-        parts(2, lambda kind, i: q_up(kind, i).wait_recv())
-
-    @pl.when(row == 3)
-    def _():
-        def forward(kind, i):
-            q_dn(kind, i).wait_recv()
-            q_dn(kind, i, qd).start()
-        parts(0, forward)
-        parts(1, forward)
-        rest_dn()
-        parts(0, lambda kind, i: q_up(kind, i).wait_recv())
-        parts(1, lambda kind, i: q_up(kind, i).wait_recv())
-        parts(2, lambda kind, i: q_dn(kind, i).wait_recv())
+    for which, choice in enumerate(choices):
+        sets[:] = choice
+
+        @pl.when(jnp.logical_and(core == which, row == 0))
+        def _():
+            parts(0, send(q_dn))
+            parts(2, send(q_up))
+            parts(1, send(q_up))
+            rest_up()
+
+            def around(kind, i):
+                q_dn(kind, i).wait_recv()
+
+                def add(x):
+                    qd[x] = qd[x] + g[x]
+                over(kind, i, add)
+                q_dn(kind, i, qd).start()
+            parts(1, around)
+            parts(2, around)
+
+        @pl.when(jnp.logical_and(core == which, row == 1))
+        def _():
+            parts(1, send(q_dn))
+            parts(0, send(q_up))
+
+            def both(kind, i):
+                q_up(kind, i).wait_recv()
+                q_dn(kind, i).wait_recv()
+
+                def add(x):
+                    own = g[x]
+                    qd[x] = qd[x] + own
+                    g[x] = qu[x] + own
+                over(kind, i, add)
+                q_up(kind, i).start()
+                q_dn(kind, i, qd).start()
+            parts(2, both)
+            rest_up()
+            rest_dn()
+            parts(1, lambda kind, i: q_up(kind, i).wait_recv())
+            parts(0, lambda kind, i: q_dn(kind, i).wait_recv())
+
+        @pl.when(jnp.logical_and(core == which, row == 2))
+        def _():
+            parts(2, send(q_dn))
+            parts(1, send(q_up))
+
+            def both(kind, i):
+                q_up(kind, i).wait_recv()
+
+                def add(x):
+                    g[x] = qu[x] + g[x]
+                over(kind, i, add)
+                q_up(kind, i).start()
+                q_dn(kind, i).wait_recv()
+                q_dn(kind, i, qd).start()
+            parts(0, both)
+            rest_up()
+            rest_dn()
+            parts(1, lambda kind, i: q_dn(kind, i).wait_recv())
+            parts(2, lambda kind, i: q_up(kind, i).wait_recv())
+
+        @pl.when(jnp.logical_and(core == which, row == 3))
+        def _():
+            def forward(kind, i):
+                q_dn(kind, i).wait_recv()
+                q_dn(kind, i, qd).start()
+            parts(0, forward)
+            parts(1, forward)
+            rest_dn()
+            parts(0, lambda kind, i: q_up(kind, i).wait_recv())
+            parts(1, lambda kind, i: q_up(kind, i).wait_recv())
+            parts(2, lambda kind, i: q_dn(kind, i).wait_recv())
 
     scale = 1.0 / (ny * rows)
+
+    cuts = [jnp.where(core == 0, choices[0][kind][0], choices[1][kind][0]) for kind in (1, 2)]
 
     def end_row(x):
         low = ylo[n % 2, x]
-        kind = (x >= sets[1][0]).astype(jnp.int32) + (x >= sets[2][0]).astype(jnp.int32)
+        kind = (x >= cuts[0]).astype(jnp.int32) + (x >= cuts[1]).astype(jnp.int32)
         use_u = jnp.logical_and(has_dn, kind != row - 1)
         use_d = jnp.logical_and(has_dn, kind <= row - 1)
         sums = lax.select(use_u, qu[x], zeros) + lax.select(use_d, qd[x], zeros)
@@ -451,14 +458,16 @@
         each(TAILS, lambda j: tail_dn(j).wait_send())
     wait_side_sends(n)
 
-    for r in range(rows):
-        @pl.when(row == r)
-        def _():
-            for kind in range(3):
-                if r < rows - 1 and kind != r:
-                    parts(kind, lambda kind, i: q_up(kind, i).wait_send())
-                if kind not in {0: (), 1: (0,), 2: (1,), 3: (2,)}[r]:
-                    parts(kind, lambda kind, i: q_dn(kind, i).wait_send())
+    for which, choice in enumerate(choices):
+        sets[:] = choice
+        for r in range(rows):
+            @pl.when(jnp.logical_and(core == which, row == r))
+            def _():
+                for kind in range(3):
+                    if r < rows - 1 and kind != r:
+                        parts(kind, lambda kind, i: q_up(kind, i).wait_send())
+                    if kind not in {0: (), 1: (0,), 2: (1,), 3: (2,)}[r]:
+                        parts(kind, lambda kind, i: q_dn(kind, i).wait_send())
 
 
 def write(c_ref, t_ref, out_c, out_t, sem):
@@ -480,7 +489,7 @@
     shape = jax.ShapeDtypeStruct(tracer.shape, jnp.float32)
     vmem = lambda *s: pltpu.VMEM(s, jnp.float32)
     dma = pltpu.SemaphoreType.DMA
-    parts = sum(count for _, count, _, _ in column_sets(nx))
+    parts = max(sum(count for _, count, _, _ in column_sets(nx, shares)) for shares in SHARES)
     sums, field = pl.pallas_call(
         functools.partial(kernel, sizes),
         out_shape=(shape, shape),

time: 223 us -> 223 us (level)
  no operation moved by 1% of the time
where the time goes in v5:
time: 223 us
  Pallas kernels  222 us (100%)
    pallas_call x1, Pallas kernels, body(): pl.pallas_call(functools.partial(kernel, sizes), out_shape=(shape, shape)...  216 us
    pallas_call x1, Pallas kernels, body(): pl.pallas_call(write, out_shape=(shape, shape), in_specs=[pl.BlockSpec(me...  5.93 us

profile of v5, /device:TPU:68, one launch (start us, length us, event | category | flops | bytes accessed | tf_op | source)
XLA Modules:
  0.0 222.9 jit_solution(12628660135906463855)
XLA Ops:
  0.6 216.3 %grid_steps.1 = (f32[4,64,64,128]{3,2,1,0:T(8,128)S(1)}, f32[4,64,64,128]{3,2,1,0:T(8,128)S(1)}) custom-call(f32[4,64,64,128]{3,2,1,0:T(8,128)} %tr.1, f32[4,64,64,128]{3,2,1,0:T(8,128)} %cr.1), custom_call_target="tpu_custom_call" | custom-call | tf_op jit(solution)/shard_map/grid_steps/pallas_call | solution.py:493
  217.0 5.9 %write_out.1 = (f32[4,64,64,128]{3,2,1,0:T(8,128)}, f32[4,64,64,128]{3,2,1,0:T(8,128)}) custom-call(f32[4,64,64,128]{3,2,1,0:T(8,128)S(1)} %get-tuple-element.4.c_ref, f32[4,64,64,128]{3,2,1,0:T(8,128)S(1)} %get-tuple-element.5.t_ref), custom_call_target="tpu_custom_call" | custom-call | tf_op jit(solution)/shard_map/write_out/pallas_call | solution.py:515

commit v6 on v5

--- a/solution.py
+++ b/solution.py
@@ -10,7 +10,7 @@
 STEPS = 4
 CHUNKS = 2
 HELD = 1
-TAILS = 4
+TAILS = 2
 WRITES = 4
 SHARES = ((21, 22, 21), (22, 21, 21))
 MESH = pl.DeviceIdType.MESH

time: 223 us -> 223 us (level)
  no operation moved by 1% of the time
where the time goes in v6:
time: 223 us
  Pallas kernels  222 us (100%)
    pallas_call x1, Pallas kernels, body(): pl.pallas_call(functools.partial(kernel, sizes), out_shape=(shape, shape)...  216 us
    pallas_call x1, Pallas kernels, body(): pl.pallas_call(write, out_shape=(shape, shape), in_specs=[pl.BlockSpec(me...  5.93 us

profile of v6, /device:TPU:68, one launch (start us, length us, event | category | flops | bytes accessed | tf_op | source)
XLA Modules:
  0.0 223.0 jit_solution(17135669575666659018)
XLA Ops:
  0.6 216.5 %grid_steps.1 = (f32[4,64,64,128]{3,2,1,0:T(8,128)S(1)}, f32[4,64,64,128]{3,2,1,0:T(8,128)S(1)}) custom-call(f32[4,64,64,128]{3,2,1,0:T(8,128)} %tr.1, f32[4,64,64,128]{3,2,1,0:T(8,128)} %cr.1), custom_call_target="tpu_custom_call" | custom-call | tf_op jit(solution)/shard_map/grid_steps/pallas_call | solution.py:493
  217.1 5.9 %write_out.1 = (f32[4,64,64,128]{3,2,1,0:T(8,128)}, f32[4,64,64,128]{3,2,1,0:T(8,128)}) custom-call(f32[4,64,64,128]{3,2,1,0:T(8,128)S(1)} %get-tuple-element.4.c_ref, f32[4,64,64,128]{3,2,1,0:T(8,128)S(1)} %get-tuple-element.5.t_ref), custom_call_target="tpu_custom_call" | custom-call | tf_op jit(solution)/shard_map/write_out/pallas_call | solution.py:515
